TPU v7x, 512 devices: a whole 4x4x16 slice. The times are simulated.
512 devices in a mesh: panel: 128 (over z, y, core), obs: 4 (over x).
Axes of the slice: x: 4, y: 4, z: 16, core: 2. Of those that a mesh axis runs over, the one named last changes fastest.
Arguments:
- flow_blocks: bfloat16 [16384, 4, 1280], P('panel'), may hold values from -6 to 6
- interp_weights: bfloat16 [512, 128, 512], P(('panel', 'obs')), may hold values from -0.25 to 0.25
- donor_owner: int32 [65536, 1], P(('panel', 'obs')), may hold values from 0 to 127; in each aligned block of 128 rows (0 to 127, 128 to 255, ...) at most 2 rows name the same one
- donor_block: int32 [65536], P(('panel', 'obs')), may hold values from 0 to 127
- panel_normals: float32 [3, 65536], P(None, ('panel', 'obs')), may hold values from -0.75 to 0.75
- panel_points: float32 [3, 65536], P(None, ('panel', 'obs')), may hold values from -1 to 1
- observer_points: float32 [3, 1024], P(None, 'obs'), may hold values from -12 to 12, as said below
Outputs:
- pressure: float32 [128, 1024], P('panel', 'obs')
Inputs may be any that keep to these rules, and one draw needn't show every extreme that they name: `donor_owner`: within the rows of one device, no owner index is named by more than 2 rows; some devices' rows name one owner exactly 2 times. `observer_points`: every observer lies between 6 and 12 from the anchor.
All inputs are finite; a program needn't handle non-finite values.
Results may differ from a plain program's by a relative error of at most 0.0003.
Values may be sent and summed in bfloat16 or wider, within the bound.
No kernel may reach another device: no remote copies, remote signals or barrier semaphores. Data moves between devices by JAX's collectives and lax.ppermute only.
A program may use at most 64 MiB of HBM per device.

v0:
```python
import math

import jax
import jax.numpy as jnp
from jax import lax
from jax.sharding import Mesh
from jax.sharding import PartitionSpec as P

NV = 5
NT = 256
HARM = 64
PANEL = ("panel_0", "panel_1", "panel_2")
PANEL_OBS = ("panel_0", "panel_1", "panel_2", "obs")


KAPPA = 0.5


def sent_together(arrays, axis, dim, along):
    ends, at = ([], 0)
    for a in arrays[:-1]:
        at += a.shape[along]
        ends.append(at)
    both = jnp.concatenate(arrays, axis=along)
    return tuple(jnp.split(lax.all_gather(both, axis, axis=dim, tiled=True), ends, axis=along))


def split_up(value, dim, count):
    dims = value.shape
    parts = value.reshape(*dims[:dim], count, dims[dim] // count, *dims[dim + 1 :])
    return jnp.moveaxis(parts, dim, 0)


def sum_at_owner(value, axis, dim):
    count = lax.axis_size(axis)
    parts = lax.all_to_all(split_up(value, dim, count), axis, 0, 0, tiled=True)
    return jnp.sum(parts, axis=0)


def sum_by_axis(value, axes, dim):
    far, near = axes
    own = sum_at_owner(split_up(value, dim, lax.axis_size(far)), near, dim + 1)
    return jnp.sum(lax.all_to_all(own, far, 0, 0, tiled=True), axis=0)


def fourier_table(samples, orders):
    sample_ids = jnp.arange(samples, dtype=jnp.int32)
    harmonic = jnp.arange(1, orders + 1, dtype=jnp.int32)
    wrapped = sample_ids[:, None] * harmonic[None, :] % samples
    angles = wrapped.astype(jnp.float32) * (2.0 * math.pi / samples)
    factor = 2.0 / samples
    return jnp.concatenate([factor * jnp.cos(angles), -factor * jnp.sin(angles)], axis=1)


def spectra_of(values, normals, transform, samples):
    panels = values.shape[0]
    fields = values.reshape(panels, NV, samples)
    density = 1.0 + fields[:, 0]
    velocity = fields[:, 1:4]
    pressure_pert = fields[:, 4]
    normal_vec = jnp.transpose(normals)[:, :, None]
    normal_flow = jnp.sum(velocity * normal_vec, axis=1)
    mass_flux = density * normal_flow
    loading = pressure_pert[:, None, :] * normal_vec + mass_flux[:, None, :] * velocity
    series = jnp.concatenate([mass_flux[:, None, :], loading], axis=1)
    return jnp.einsum("pct,tk->ckp", series, transform, precision=lax.Precision.HIGHEST)


def doubled(base_phase, orders):
    cosines = jnp.cos(base_phase)[None]
    sines = jnp.sin(base_phase)[None]
    while cosines.shape[0] < orders:
        last_cos = cosines[-1]
        last_sin = sines[-1]
        cosines, sines = (
            jnp.concatenate([cosines, cosines * last_cos - sines * last_sin], axis=0),
            jnp.concatenate([sines, sines * last_cos + cosines * last_sin], axis=0),
        )
    return (cosines, sines)


def radiate(spectra, points, observers):
    orders = spectra.shape[1] // 2
    offset_vec = observers[:, None, :] - points[:, :, None]
    distance = jnp.sqrt(jnp.sum(offset_vec * offset_vec, axis=0))
    inverse = 1.0 / distance
    direction = offset_vec * inverse[None]
    wavenum = (KAPPA * jnp.arange(1, orders + 1, dtype=jnp.float32))[:, None, None]
    load_re = (
        spectra[1, :orders][:, :, None] * direction[0][None]
        + spectra[2, :orders][:, :, None] * direction[1][None]
        + spectra[3, :orders][:, :, None] * direction[2][None]
    )
    load_im = (
        spectra[1, orders:][:, :, None] * direction[0][None]
        + spectra[2, orders:][:, :, None] * direction[1][None]
        + spectra[3, orders:][:, :, None] * direction[2][None]
    )
    amp_re = load_re * inverse[None] - wavenum * (spectra[0, orders:][:, :, None] + load_im)
    amp_im = load_im * inverse[None] + wavenum * (spectra[0, :orders][:, :, None] + load_re)
    cosines, sines = doubled(KAPPA * distance, orders)
    spreading = (inverse / (4.0 * math.pi))[None]
    real_part = jnp.sum((amp_re * cosines + amp_im * sines) * spreading, axis=1)
    imag_part = jnp.sum((amp_im * cosines - amp_re * sines) * spreading, axis=1)
    return jnp.concatenate([real_part, imag_part], axis=0)


def radiate_all(spectra, points, observers):
    panel_total = spectra.shape[1]
    block_size = math.gcd(panel_total, max(1, 32768 // observers.shape[1]))
    block_count = panel_total // block_size

    def one_block(block_index, running):
        first_panel = block_index * block_size
        block_spectra = lax.dynamic_slice_in_dim(spectra, first_panel, block_size, 1)
        block_points = lax.dynamic_slice_in_dim(points, first_panel, block_size, 1)
        return running + radiate(block_spectra.reshape(4, -1, block_size), block_points, observers)

    initial = jnp.zeros((spectra.shape[0] // 4, observers.shape[1]), jnp.float32)
    return lax.fori_loop(0, block_count, one_block, initial)


def body(
    flow_blocks,
    interp_weights,
    donor_owner,
    donor_block,
    panel_normals,
    panel_points,
    observer_points,
):
    peer_count = lax.axis_size(PANEL)
    tile_count, tile_width, stencil = interp_weights.shape
    cell_count = flow_blocks.shape[1]
    slot_count = stencil // cell_count
    row_count = tile_count * slot_count
    capacity = max(2, (3 * row_count + 2 * peer_count - 1) // (2 * peer_count))
    owner_of = donor_owner[:, 0]
    matches = (owner_of[:, None] == jnp.arange(peer_count, dtype=jnp.int32)[None, :]).astype(
        jnp.int32
    )
    slot_rank = jnp.sum(jnp.cumsum(matches, axis=0) * matches, axis=1) - 1
    requests = jnp.zeros((peer_count, capacity), jnp.int32).at[owner_of, slot_rank].set(donor_block)
    found = jnp.take(
        flow_blocks,
        lax.all_to_all(requests, PANEL, split_axis=0, concat_axis=0, tiled=True),
        axis=0,
    )
    arrived = lax.all_to_all(found, PANEL, split_axis=0, concat_axis=0, tiled=True)
    history = arrived.shape[-1]
    flat_rows = arrived.reshape(peer_count * capacity, cell_count, history)
    picked = jnp.take(flat_rows, owner_of * capacity + slot_rank, axis=0)
    donors = picked.reshape(tile_count, stencil, history)
    values = jnp.einsum("tpc,tcv->tpv", interp_weights, donors, preferred_element_type=jnp.float32)
    values = values.reshape(tile_count * tile_width, history)
    transform = fourier_table(NT, HARM)
    spectra = spectra_of(values, panel_normals, transform, NT).reshape(8 * HARM, -1)
    group_spectra, group_points = sent_together((spectra, panel_points), "obs", 1, 0)
    partial_sum = radiate_all(group_spectra, group_points, observer_points)
    pressure = sum_by_axis(partial_sum, (("panel_0", "panel_1"), "panel_2"), 0)
    return pressure


def solution(mesh):
    finer = Mesh(
        mesh.devices.reshape(16, 4, 2, mesh.shape["obs"]), ("panel_0", "panel_1", "panel_2", "obs")
    )
    in_specs = (
        P(PANEL, None, None),
        P(PANEL_OBS, None, None),
        P(PANEL_OBS, None),
        P(PANEL_OBS),
        P(None, PANEL_OBS),
        P(None, PANEL_OBS),
        P(None, "obs"),
    )
    out_specs = P(PANEL, "obs")
    return jax.shard_map(body, mesh=finer, in_specs=in_specs, out_specs=out_specs, check_vma=False)
```

profile of v0, /device:TPU:1, one launch (start us, length us, event | category | flops | bytes accessed | tf_op | source)
XLA Modules:
  0.0 387.0 jit_solution(17603517046210613047)
XLA Ops:
  6.5 0.8 fusion.25
  7.6 0.8 select_reduce_fusion
  8.4 0.7 fusion.30
  9.1 11.0 %scatter_fusion = s32[128,2]{0,1:T(2,128)S(1)} fusion(s32[128,2]{0,1:T(2,128)S(1)} %broadcast_in_dim.61, s32[128]{0:T(128)S(1)} %fusion.30, s32[128]{0:T(128)} %param.12), kind=kCustom, calls=%fused_computation.2 | custom fusion | bytes 2560 | tf_op jit(solution)/shard_map/scatter | solution.py:143
  20.2 35.2 %all_to_all.30 = s32[128,1,2]{2,1,0:T(1,128)S(1)} all-to-all(s32[128,1,2]{2,1,0:T(1,128)S(1)} %copy.30), channel_id=1, replica_groups=mesh['panel_0'=16,'panel_1'=4,'panel_2'=2,'obs'=4] {'panel_0','panel_1',..., dimensions={0} | all-to-all | bytes 2048 | tf_op jit(solution)/shard_map/all_to_all | solution.py:146
  55.8 4.2 %gather_fusion = bf16[256,4,1280]{2,1,0:T(4,128)(2,1)} fusion(bf16[128,4,1280]{2,1,0:T(4,128)(2,1)S(1)} %copy-done, s32[1024]{0:T(1024)S(1)} %pad_clamp_fusion.1), kind=kCustom, calls=%fused_computation | custom fusion | bytes 5243904 | tf_op jit(solution)/shard_map/jit(_take)/gather | solution.py:144
  60.0 4.6 %broadcast_select_fusion = bf16[128,2,4,1280]{3,2,1,0:T(4,128)(2,1)} fusion(bf16[128,2,4,1280]{3,2,1,0:T(4,128)(2,1)} %bitcast.166, pred[128,2]{1,0:T(8,128)(4,1)S(1)} %copy.32), kind=kLoop, calls=%fused_computation.95 | loop fusion | flops 1310720 | bytes 5243136 | tf_op jit(solution)/shard_map/jit(_take)/select_n | solution.py:144
  64.6 6.8 %all-to-all-start.1 = ((bf16[128,2,4,1280]{3,2,1,0:T(4,128)(2,1)}), bf16[128,2,4,1280]{3,2,1,0:T(4,128)(2,1)}, u32[]{:S(2)}, u32[]{:S(2)}) async-start(bf16[128,2,4,1280]{3,2,1,0:T(4,128)(2,1)} %broadcast_select_fusion), calls=%async_computation.1 | async-start | bytes 5242880 | tf_op jit(solution)/shard_map/all_to_all | solution.py:149
  72.1 117.7 %all-to-all-done.1 = bf16[128,2,4,1280]{3,2,1,0:T(4,128)(2,1)} async-done(((bf16[128,2,4,1280]{3,2,1,0:T(4,128)(2,1)}), bf16[128,2,4,1280]{3,2,1,0:T(4,128)(2,1)}, u32[]{:S(2)}, u32[]{:S(2)}) %all-to-all-start.1) | async-done | bytes 2621472 | tf_op jit(solution)/shard_map/all_to_all | solution.py:149
  189.8 4.4 %gather_fusion.1 = bf16[128,4,1280]{2,1,0:T(4,128)(2,1)} fusion(bf16[256,4,1280]{2,1,0:T(4,128)(2,1)} %bitcast.10, s32[1024]{0:T(1024)S(1)} %pad_clamp_fusion), kind=kCustom, calls=%fused_computation.1 | custom fusion | bytes 2621952 | tf_op jit(solution)/shard_map/jit(_take)/gather | solution.py:152
  194.2 2.0 broadcast_select_fusion.1
  196.2 1.3 select_n.80
  197.5 1.9 fusion.20
  200.8 0.7 pad_maximum_fusion.6
  201.5 27.3 %all-gather.2.cloned.1.call-done = f32[515,512]{1,0:T(8,128)} async-done(((f32[515,128]{1,0:T(8,128)}), f32[515,512]{1,0:T(8,128)}) %all-gather.2.cloned.1.call-update) | async-done | bytes 1054736 | tf_op jit(solution)/shard_map/all_gather | solution.py:25
  228.8 2.3 split.8
  231.1 0.7 split.9
  231.8 111.7 %while.14 = (s32[]{:T(128)}, f32[128,256]{1,0:T(8,128)}, f32[512,512]{1,0:T(8,128)}, f32[3,256]{1,0:T(4,128)S(1)}, f32[3,512]{1,0:T(4,128)S(1)}, /*index=5*/s32[]{:T(128)}, s32[]{:T(128)}, s32[]{:T(128)}, s32[]{:T(128)}) while((s32[]{:T(128)}, f32[128,256]{1,0:T(8,128)}, f32[512,512]{1,0:T(8,128)}, f32[3,256]{1,0:T(4,128)S(1)}, ...), condition=%wide.region_8.9_spmd.clone, body=%wide.region_4.8_spmd.clone.sunk | while | flops 76873856 | bytes 116667128 | solution.py:120
  235.4 1.7 copy-done.1
  237.1 0.7 copy-done.2
  237.8 3.4 constant_dynamic-update-slice_fusion.42
  241.7 0.7 slice_bitcast_fusion.34
  243.1 4.2 %subtract_dynamic-update-slice_fusion.2 = (f32[64,128,256]{2,1,0:T(8,128)S(1)}, f32[64,128,256]{2,1,0:T(8,128)S(1)}) fusion(f32[64,128,256]{2,1,0:T(8,128)S(1)} %get-tuple-element.343, f32[32,128,256]{2,1,0:T(8,128)} %get-tuple-element.344, f32[32,128,256]{2,1,0:T(8,128)S(1)} %constant_dynamic-update-slice_fusion.43, ...), kind=kLoop, calls=%fused_computation.10.clone.1 | loop fusion | flops 6291456 | bytes 17039360 | tf_op jit(solution)/shard_map/while/body/eval_jaxpr/concatenate | solution.py:76
  247.4 1.0 constant_dynamic-slice_fusion.5
  248.4 10.6 %multiply_reduce_fusion.4 = (f32[64,256]{1,0:T(8,128)S(1)}, f32[64,256]{1,0:T(8,128)S(1)}) fusion(f32[64,128,256]{2,1,0:T(8,128)S(1)} %get-tuple-element.349, f32[64,128,256]{2,1,0:T(8,128)S(1)} %get-tuple-element.350, f32[128,256]{1,0:T(8,128)S(1)} %get-tuple-element.351, f32[64,128]{1,0:T(8,128)S(1)} %get-tuple-element.352, ...), kind=kLoop, calls=%fused_computation.4.clone.1 | loop fusion | flops 58687488 | bytes 17826048 | tf_op jit(solution)/shard_map/while/body/eval_jaxpr/reduce_sum | solution.py:103
  263.3 1.7 copy-done.1
  265.1 0.7 copy-done.2
  265.8 3.4 constant_dynamic-update-slice_fusion.42
  269.7 0.7 slice_bitcast_fusion.34
  271.0 4.2 %subtract_dynamic-update-slice_fusion.2 = (f32[64,128,256]{2,1,0:T(8,128)S(1)}, f32[64,128,256]{2,1,0:T(8,128)S(1)}) fusion(f32[64,128,256]{2,1,0:T(8,128)S(1)} %get-tuple-element.343, f32[32,128,256]{2,1,0:T(8,128)} %get-tuple-element.344, f32[32,128,256]{2,1,0:T(8,128)S(1)} %constant_dynamic-update-slice_fusion.43, ...), kind=kLoop, calls=%fused_computation.10.clone.1 | loop fusion | flops 6291456 | bytes 17039360 | tf_op jit(solution)/shard_map/while/body/eval_jaxpr/concatenate | solution.py:76
  275.3 1.0 constant_dynamic-slice_fusion.5
  276.4 10.6 %multiply_reduce_fusion.4 = (f32[64,256]{1,0:T(8,128)S(1)}, f32[64,256]{1,0:T(8,128)S(1)}) fusion(f32[64,128,256]{2,1,0:T(8,128)S(1)} %get-tuple-element.349, f32[64,128,256]{2,1,0:T(8,128)S(1)} %get-tuple-element.350, f32[128,256]{1,0:T(8,128)S(1)} %get-tuple-element.351, f32[64,128]{1,0:T(8,128)S(1)} %get-tuple-element.352, ...), kind=kLoop, calls=%fused_computation.4.clone.1 | loop fusion | flops 58687488 | bytes 17826048 | tf_op jit(solution)/shard_map/while/body/eval_jaxpr/reduce_sum | solution.py:103
  291.2 1.7 copy-done.1
  293.0 0.7 copy-done.2
  293.7 3.4 constant_dynamic-update-slice_fusion.42
  297.6 0.7 slice_bitcast_fusion.34
  298.9 4.2 %subtract_dynamic-update-slice_fusion.2 = (f32[64,128,256]{2,1,0:T(8,128)S(1)}, f32[64,128,256]{2,1,0:T(8,128)S(1)}) fusion(f32[64,128,256]{2,1,0:T(8,128)S(1)} %get-tuple-element.343, f32[32,128,256]{2,1,0:T(8,128)} %get-tuple-element.344, f32[32,128,256]{2,1,0:T(8,128)S(1)} %constant_dynamic-update-slice_fusion.43, ...), kind=kLoop, calls=%fused_computation.10.clone.1 | loop fusion | flops 6291456 | bytes 17039360 | tf_op jit(solution)/shard_map/while/body/eval_jaxpr/concatenate | solution.py:76
  303.2 1.0 constant_dynamic-slice_fusion.5
  304.3 10.6 %multiply_reduce_fusion.4 = (f32[64,256]{1,0:T(8,128)S(1)}, f32[64,256]{1,0:T(8,128)S(1)}) fusion(f32[64,128,256]{2,1,0:T(8,128)S(1)} %get-tuple-element.349, f32[64,128,256]{2,1,0:T(8,128)S(1)} %get-tuple-element.350, f32[128,256]{1,0:T(8,128)S(1)} %get-tuple-element.351, f32[64,128]{1,0:T(8,128)S(1)} %get-tuple-element.352, ...), kind=kLoop, calls=%fused_computation.4.clone.1 | loop fusion | flops 58687488 | bytes 17826048 | tf_op jit(solution)/shard_map/while/body/eval_jaxpr/reduce_sum | solution.py:103
  319.2 1.7 copy-done.1
  320.9 0.7 copy-done.2
  321.6 3.4 constant_dynamic-update-slice_fusion.42
  326.8 4.2 %subtract_dynamic-update-slice_fusion.2 = (f32[64,128,256]{2,1,0:T(8,128)S(1)}, f32[64,128,256]{2,1,0:T(8,128)S(1)}) fusion(f32[64,128,256]{2,1,0:T(8,128)S(1)} %get-tuple-element.343, f32[32,128,256]{2,1,0:T(8,128)} %get-tuple-element.344, f32[32,128,256]{2,1,0:T(8,128)S(1)} %constant_dynamic-update-slice_fusion.43, ...), kind=kLoop, calls=%fused_computation.10.clone.1 | loop fusion | flops 6291456 | bytes 17039360 | tf_op jit(solution)/shard_map/while/body/eval_jaxpr/concatenate | solution.py:76
  331.2 1.0 constant_dynamic-slice_fusion.5
  332.2 10.6 %multiply_reduce_fusion.4 = (f32[64,256]{1,0:T(8,128)S(1)}, f32[64,256]{1,0:T(8,128)S(1)}) fusion(f32[64,128,256]{2,1,0:T(8,128)S(1)} %get-tuple-element.349, f32[64,128,256]{2,1,0:T(8,128)S(1)} %get-tuple-element.350, f32[128,256]{1,0:T(8,128)S(1)} %get-tuple-element.351, f32[64,128]{1,0:T(8,128)S(1)} %get-tuple-element.352, ...), kind=kLoop, calls=%fused_computation.4.clone.1 | loop fusion | flops 58687488 | bytes 17826048 | tf_op jit(solution)/shard_map/while/body/eval_jaxpr/reduce_sum | solution.py:103
  343.5 1.0 reshape_reshape.7
  344.5 6.1 %all_to_all.31 = f32[2,64,1,256]{3,1,2,0:T(8,128)S(1)} all-to-all(f32[2,64,1,256]{3,1,2,0:T(8,128)S(1)} %copy.36), channel_id=1, replica_groups=mesh['panel_0'=16,'panel_1'=4,'panel_2'=2,'obs'=4] {'panel_2'}, dimensions={0} | all-to-all | bytes 262144 | tf_op jit(solution)/shard_map/all_to_all | solution.py:36
  350.6 28.8 %all_to_all.32 = f32[64,1,256]{2,1,0:T(1,128)S(1)} all-to-all(f32[64,1,256]{2,1,0:T(1,128)S(1)} %reduce_sum.85), channel_id=1, replica_groups=mesh['panel_0'=16,'panel_1'=4,'panel_2'=2,'obs'=4] {'panel_0','panel_1'}, dimensions={0} | all-to-all | bytes 131072 | tf_op jit(solution)/shard_map/all_to_all | solution.py:43
  (178 shorter events, 25.6 us)
Async XLA Ops:
  6.5 49.3 %copy-start = (bf16[128,4,1280]{2,1,0:T(4,128)(2,1)S(1)}, bf16[128,4,1280]{2,1,0:T(4,128)(2,1)}, u32[]{:S(2)}) copy-start(bf16[128,4,1280]{2,1,0:T(4,128)(2,1)} %param.9) | copy-start | bytes 3932164
  60.0 11.6 %copy-start.8 = (s32[128,1]{0,1:T(1,128)S(1)}, s32[128,1]{0,1:T(1,128)}, u32[]{:S(2)}) copy-start(s32[128,1]{0,1:T(1,128)} %param.11) | copy-start | bytes 1540
  64.6 125.2 %all-to-all-start.1 = ((bf16[128,2,4,1280]{3,2,1,0:T(4,128)(2,1)}), bf16[128,2,4,1280]{3,2,1,0:T(4,128)(2,1)}, u32[]{:S(2)}, u32[]{:S(2)}) async-start(bf16[128,2,4,1280]{3,2,1,0:T(4,128)(2,1)} %broadcast_select_fusion), calls=%async_computation.1 | async-start | bytes 5242880 | tf_op jit(solution)/shard_map/all_to_all | solution.py:149
  71.4 126.1 %copy-start.6 = (bf16[1,128,512]{2,1,0:T(8,128)(2,1)S(1)}, bf16[1,128,512]{2,1,0:T(8,128)(2,1)}, u32[]{:S(2)}) copy-start(bf16[1,128,512]{2,1,0:T(8,128)(2,1)} %param.10) | copy-start | bytes 393220
  71.4 157.4 %all-gather.2.cloned.1.call-start = ((), (), s32[]{:S(2)}) async-start(), calls=%async_computation.4 | async-start | bytes 1331200 | tf_op jit(solution)/shard_map/all_gather | solution.py:25
  196.2 3.6 copy-start.7
  197.5 3.3 copy-start.9
  199.4 32.4 %copy-start.5 = (f32[3,256]{1,0:T(4,128)S(1)}, f32[3,256]{1,0:T(4,128)}, u32[]{:S(2)}) copy-start(f32[3,256]{1,0:T(4,128)} %param.15) | copy-start | bytes 9220
  235.2 2.0 copy-start.1
  235.3 2.5 copy-start.2
  248.4 10.6 %copy-start.3 = (f32[128,256]{1,0:T(8,128)S(1)}, f32[128,256]{1,0:T(8,128)}, u32[]{:S(2)}) copy-start(f32[128,256]{1,0:T(8,128)} %get-tuple-element.376) | copy-start | bytes 393220 | tf_op jit(solution)/shard_map/while
  259.1 0.7 copy-start.4
  263.1 2.0 copy-start.1
  263.3 2.5 copy-start.2
  276.3 10.6 %copy-start.3 = (f32[128,256]{1,0:T(8,128)S(1)}, f32[128,256]{1,0:T(8,128)}, u32[]{:S(2)}) copy-start(f32[128,256]{1,0:T(8,128)} %get-tuple-element.376) | copy-start | bytes 393220 | tf_op jit(solution)/shard_map/while
  287.0 0.7 copy-start.4
  291.0 2.0 copy-start.1
  291.2 2.5 copy-start.2
  304.3 10.6 %copy-start.3 = (f32[128,256]{1,0:T(8,128)S(1)}, f32[128,256]{1,0:T(8,128)}, u32[]{:S(2)}) copy-start(f32[128,256]{1,0:T(8,128)} %get-tuple-element.376) | copy-start | bytes 393220 | tf_op jit(solution)/shard_map/while
  314.9 0.7 copy-start.4
  319.0 2.0 copy-start.1
  319.1 2.5 copy-start.2
  332.2 10.6 %copy-start.3 = (f32[128,256]{1,0:T(8,128)S(1)}, f32[128,256]{1,0:T(8,128)}, u32[]{:S(2)}) copy-start(f32[128,256]{1,0:T(8,128)} %get-tuple-element.376) | copy-start | bytes 393220 | tf_op jit(solution)/shard_map/while
  342.8 0.7 copy-start.4
Sparse Core Ops, SparseCore 0:
  201.6 27.0 all-gather.1
where the time goes:
time: 388 us; the launch traced here: 387 us
  waiting for transfers between devices  145 us (37%)
  other arithmetic  96.1 us (25%)
  blocking collectives  70.2 us (18%)
  local copies, waits for them, and re-layouts  51.5 us (13%)
  between operations  13.7 us (4%)
  starting transfers between devices  6.99 us (2%)
    all_to_all x1, waiting for transfers between devices, body(): lax.all_to_all(found, PANEL, split_axis=0, concat_axis=0, tiled=True)  118 us
    reduce_sum x4, other arithmetic, radiate(): real_part = jnp.sum((amp_re * cosines + amp_im * sines) * spreading, axis=1)  42.2 us
    all_to_all x1, blocking collectives, body(): lax.all_to_all(requests, PANEL, split_axis=0, concat_axis=0, tiled=True)  35.2 us
    all_to_all x1, blocking collectives, sum_by_axis(): return jnp.sum(lax.all_to_all(own, far, 0, 0, tiled=True), axis=0)  28.8 us
    all_gather x1, waiting for transfers between devices, sent_together(): lax.all_gather(both, axis, axis=dim, tiled=True)  27.3 us
    while x36, other arithmetic  22.6 us
    concatenate x4, other arithmetic, doubled(): jnp.concatenate([cosines, cosines * last_cos - sines * last_sin], axis=0)  16.6 us
    while x44, local copies, waits for them, and re-layouts  14.6 us
  transfers between devices with their start and end apart: 2, of which 2 were waited for; matrix products, arithmetic and copies ran while one was open for 0% of the time, Pallas kernels for 0%

commit v1 on v0

v1 whole, which is shorter than its diff:
```python
import functools
import math

import jax
import jax.numpy as jnp
from jax import lax
from jax.experimental import pallas as pl
from jax.experimental.pallas import tpu as pltpu
from jax.sharding import Mesh
from jax.sharding import PartitionSpec as P

NV = 5
NT = 256
HARM = 64
KAPPA = 0.5
PANEL = ("z", "y", "c")
SLAB = ("y", "c", "x")
CAP = 2
GROUP = 8
PANEL_STEP = 8
OBS_TILE = 256


def fourier_table(samples, orders):
    sample_ids = jnp.arange(samples, dtype=jnp.int32)
    harmonic = jnp.arange(1, orders + 1, dtype=jnp.int32)
    wrapped = sample_ids[:, None] * harmonic[None, :] % samples
    angles = wrapped.astype(jnp.float32) * (2.0 * math.pi / samples)
    factor = 2.0 / samples
    return jnp.concatenate([factor * jnp.cos(angles), -factor * jnp.sin(angles)], axis=1)


def geometry_kernel(points_ref, observers_ref, basis_ref, cos_ref, sin_ref):
    panels = points_ref.shape[0]
    offsets = [observers_ref[i : i + 1, :] - points_ref[:, i : i + 1] for i in range(3)]
    distance = jnp.sqrt(offsets[0] * offsets[0] + offsets[1] * offsets[1] + offsets[2] * offsets[2])
    inverse = 1.0 / distance
    weight = inverse * (1.0 / (4.0 * math.pi))
    near = weight * inverse
    rows = lambda j: pl.ds(j, panels, stride=GROUP)
    for i in range(3):
        direction = offsets[i] * inverse
        basis_ref[rows(i), :] = direction * near
        basis_ref[rows(3 + i), :] = direction * weight
    basis_ref[rows(6), :] = weight
    basis_ref[rows(7), :] = jnp.zeros_like(weight)
    phase = KAPPA * distance
    c1, s1 = jnp.cos(phase), jnp.sin(phase)
    c, s = [c1], [s1]
    for m in range(2, GROUP + 1):
        a, b = (m // 2, m - m // 2)
        ca, sa, cb, sb = c[a - 1], s[a - 1], c[b - 1], s[b - 1]
        c.append(ca * cb - sa * sb)
        s.append(sa * cb + ca * sb)
    for m in range(GROUP):
        cos_ref[rows(m), :] = c[m]
        sin_ref[rows(m), :] = s[m]


def geometry(points, observers):
    panels, total = points.shape[0], observers.shape[1]
    tile = 128
    shape = jax.ShapeDtypeStruct((panels * GROUP, total), jnp.float32)
    spec = pl.BlockSpec((panels * GROUP, tile), lambda x: (0, x))
    return pl.pallas_call(
        geometry_kernel,
        grid=(total // tile,),
        out_shape=(shape, shape, shape),
        in_specs=[
            pl.BlockSpec((panels, 3), lambda x: (0, 0)),
            pl.BlockSpec((3, tile), lambda x: (0, x)),
        ],
        out_specs=(spec, spec, spec),
        cost_estimate=pl.CostEstimate(
            flops=200 * panels * total, bytes_accessed=12 * panels * GROUP * total, transcendentals=3 * panels * total
        ),
        name="geometry",
    )(points, observers)


def split_two(value):
    high = value.astype(jnp.bfloat16).astype(jnp.float32)
    return high, value - high


def fill_factors(values_ref, normals_ref, table_ref, factors_ref):
    panels = values_ref.shape[0]
    field = lambda v: values_ref[:, v * NT : (v + 1) * NT]
    normal = [normals_ref[:, i : i + 1] for i in range(3)]
    flow = field(1) * normal[0] + field(2) * normal[1] + field(3) * normal[2]
    mass = (1.0 + field(0)) * flow
    loads = [field(4) * normal[i] + mass * field(1 + i) for i in range(3)]
    series = jnp.concatenate([mass] + loads, axis=0)
    spectra = jnp.dot(series, table_ref[...], precision=lax.Precision.HIGHEST, preferred_element_type=jnp.float32)
    lane = lax.broadcasted_iota(jnp.int32, (panels, 2 * HARM), 1)
    order = (jnp.where(lane < HARM, lane, lane - HARM) + 1).astype(jnp.float32) * KAPPA
    wave = jnp.where(lane < HARM, -order, order)
    rows = lambda j: pl.ds(j, panels, stride=GROUP)
    for i in range(4):
        part = spectra[i * panels : (i + 1) * panels]
        turned = jnp.concatenate([part[:, HARM:], part[:, :HARM]], axis=1) * wave
        if i == 0:
            factors_ref[rows(6), :] = turned
        else:
            factors_ref[rows(i - 1), :] = part
            factors_ref[rows(2 + i), :] = turned
    factors_ref[rows(7), :] = jnp.zeros((panels, 2 * HARM), jnp.float32)


def radiate_kernel(values_ref, normals_ref, table_ref, basis_ref, cos_ref, sin_ref, out_ref, factors_ref):
    step = pl.program_id(0)

    @pl.when(step == 0)
    def _():
        fill_factors(values_ref, normals_ref, table_ref, factors_ref)
        out_ref[...] = jnp.zeros_like(out_ref)

    observers = out_ref.shape[1]
    together = 2

    def some_panels(turn, carry):
        local = [pl.multiple_of((turn * together + k) * GROUP, GROUP) for k in range(together)]
        lefts, rights = [], []
        for k in range(together):
            at = pl.multiple_of(step * (PANEL_STEP * GROUP) + local[k], GROUP)
            high, low = split_two(factors_ref[pl.ds(at, GROUP), :])
            lefts.append(jnp.concatenate([high, high, low, jnp.zeros_like(low)], axis=0).astype(jnp.bfloat16))
        for x in range(observers // OBS_TILE):
            lanes = slice(x * OBS_TILE, (x + 1) * OBS_TILE)
            amps, states = [], []
            for k in range(together):
                high, low = split_two(basis_ref[pl.ds(local[k], GROUP), lanes])
                right = jnp.concatenate([high, low, high, jnp.zeros_like(low)], axis=0).astype(jnp.bfloat16)
                amps.append(
                    lax.dot_general(lefts[k], right, (((0,), (0,)), ((), ())), preferred_element_type=jnp.float32)
                )
                c = cos_ref[pl.ds(local[k], GROUP), lanes]
                s = sin_ref[pl.ds(local[k], GROUP), lanes]
                c8 = jnp.broadcast_to(c[GROUP - 1 : GROUP, :], c.shape)
                s8 = jnp.broadcast_to(s[GROUP - 1 : GROUP, :], s.shape)
                states.append((c, s, c * c8 + s * s8, s * c8 - c * s8, 2.0 * c8))
            for g in range(HARM // GROUP):
                re = slice(g * GROUP, (g + 1) * GROUP)
                im = slice(HARM + g * GROUP, HARM + (g + 1) * GROUP)
                total_re, total_im = out_ref[re, lanes], out_ref[im, lanes]
                for k in range(together):
                    c, s, before_c, before_s, twice = states[k]
                    a_re, a_im = amps[k][re, :], amps[k][im, :]
                    total_re = total_re + (a_re * c + a_im * s)
                    total_im = total_im + (a_im * c - a_re * s)
                    states[k] = (twice * c - before_c, twice * s - before_s, c, s, twice)
                out_ref[re, lanes] = total_re
                out_ref[im, lanes] = total_im
        return carry

    lax.fori_loop(0, PANEL_STEP // together, some_panels, 0)


def radiate(values, normals, table, basis, cosines, sines):
    panels, observers = values.shape[0], basis.shape[1]
    whole = lambda a: pl.BlockSpec(a.shape, lambda p: (0,) * a.ndim)
    rows = pl.BlockSpec((PANEL_STEP * GROUP, observers), lambda p: (p, 0))
    return pl.pallas_call(
        radiate_kernel,
        grid=(panels // PANEL_STEP,),
        out_shape=jax.ShapeDtypeStruct((2 * HARM, observers), jnp.float32),
        in_specs=[whole(values), whole(normals), whole(table), rows, rows, rows],
        out_specs=pl.BlockSpec((2 * HARM, observers), lambda p: (0, 0)),
        scratch_shapes=[pltpu.VMEM((panels * GROUP, 2 * HARM), jnp.float32)],
        cost_estimate=pl.CostEstimate(
            flops=30 * panels * HARM * observers, bytes_accessed=12 * panels * GROUP * observers, transcendentals=0
        ),
        name="radiate",
    )(values, normals, table, basis, cosines, sines)


def body(flow_blocks, interp_weights, donor_owner, donor_block, panel_normals, panel_points, observer_points):
    peers = lax.axis_size(PANEL)
    cells, history = flow_blocks.shape[1:]
    width = interp_weights.shape[1]
    slots = donor_block.shape[0]
    owner = donor_owner[:, 0]

    row = jnp.arange(slots, dtype=jnp.int32)
    same = (owner[:, None] == owner[None, :]) & (row[None, :] < row[:, None])
    rank = jnp.sum(same.astype(jnp.int32), axis=1)
    slot = owner * CAP + rank
    slot_ids = jnp.arange(peers * CAP, dtype=jnp.int32)
    chosen = slot[:, None] == slot_ids[None, :]
    requests = jnp.sum(jnp.where(chosen, donor_block[:, None], 0), axis=0).reshape(peers, CAP)
    asked = lax.all_to_all(requests, PANEL, 0, 0, tiled=True)
    found = flow_blocks.at[asked.reshape(-1)].get(mode="promise_in_bounds")
    found = found.reshape(peers, CAP, cells, history)
    arrived = lax.all_to_all(found, PANEL, 0, 0, tiled=True)

    observers = lax.all_gather(lax.optimization_barrier((observer_points, asked))[0], "x", axis=1, tiled=True)
    basis, cosines, sines = geometry(panel_points.T, observers)
    table = fourier_table(NT, HARM)
    placing = chosen.astype(jnp.bfloat16)
    weights = interp_weights.reshape(width, slots, cells)
    placed = jnp.einsum("prc,rs->psc", weights, placing, preferred_element_type=jnp.float32)
    placed = placed.astype(jnp.bfloat16).reshape(width, peers * CAP * cells)

    values = jnp.dot(placed, arrived.reshape(-1, history), preferred_element_type=jnp.float32)
    partial = radiate(values, panel_normals.T, table, basis, cosines, sines)

    far, near, across = lax.axis_size("z"), lax.axis_size(("y", "c")), lax.axis_size("x")
    parts = partial.reshape(far, near, across, -1).transpose(1, 2, 0, 3).reshape(near * across, far, -1)
    parts = jnp.sum(lax.all_to_all(parts, SLAB, 0, 0, tiled=True), axis=0)
    parts = lax.all_to_all(parts.reshape(far, 1, -1), "z", 0, 0, tiled=True)
    return jnp.sum(parts, axis=0)


def solution(mesh):
    panel, obs = mesh.shape["panel"], mesh.shape["obs"]
    finer = Mesh(mesh.devices.reshape(panel // 8, 4, 2, obs), ("z", "y", "c", "x"))
    every = PANEL + ("x",)
    in_specs = (
        P(PANEL, None, None),
        P(every, None, None),
        P(every, None),
        P(every),
        P(None, every),
        P(None, every),
        P(None, "x"),
    )
    return jax.shard_map(body, mesh=finer, in_specs=in_specs, out_specs=P(PANEL, "x"), check_vma=False)
```

time: 388 us -> 247 us (0.64)
  other arithmetic: 96.1 us -> 5.13 us
  waiting for transfers between devices: 145 us -> 95.6 us
  Pallas kernels: 0 us -> 39.5 us
  local copies, waits for them, and re-layouts: 51.5 us -> 13.4 us
  between operations: 13.7 us -> 0.13 us
  blocking collectives: 70.2 us -> 82.3 us
    reduce_sum x12 -> x4, other arithmetic: 44.3 us -> 2.35 us  [the longest x1 0.94 us: body(): rank = jnp.sum(same.astype(jnp.int32), axis=1)]
    pallas_call x0 -> x2, Pallas kernels: none -> 39.5 us  [the longest x1 31 us: radiate(): pl.pallas_call(radiate_kernel, grid=(panels // PANEL_STEP,), out_shape=ja...]
    all_gather x1 -> x0, waiting for transfers between devices: 27.3 us -> none  [sent_together(): lax.all_gather(both, axis, axis=dim, tiled=True)]
    while x36 -> x0, other arithmetic: 22.6 us -> none
    all_to_all x1, waiting for transfers between devices: 118 us -> 95.6 us  [body(): arrived = lax.all_to_all(found, PANEL, 0, 0, tiled=True)]
    concatenate x6 -> x1, other arithmetic: 18 us -> 0.76 us  [fourier_table(): jnp.concatenate([factor * jnp.cos(angles), -factor * jnp.sin(angles)], ax...]
    while x44 -> x0, local copies, waits for them, and re-layouts: 14.6 us -> none
    scatter x1 -> x0, local copies, waits for them, and re-layouts: 11 us -> none  [body(): jnp.zeros((peer_count, capacity), jnp.int32).at[owner_of, slot_rank]]
  transfers between devices with their start and end apart: 2 -> 1, of which waited for: 2 -> 1; matrix products, arithmetic and copies ran while one was open for 0% -> 1% of each run, Pallas kernels for 0% -> 3%
where the time goes in v1:
time: 247 us; the launch traced here: 246 us
  waiting for transfers between devices  95.6 us (39%)
  blocking collectives  82.3 us (33%)
  Pallas kernels  39.5 us (16%)
  local copies, waits for them, and re-layouts  13.4 us (5%)
  starting transfers between devices  6.91 us (3%)
  other arithmetic  5.13 us (2%)
  matrix products  3.37 us (1%)
    all_to_all x1, waiting for transfers between devices, body(): arrived = lax.all_to_all(found, PANEL, 0, 0, tiled=True)  95.6 us
    all_to_all x1, blocking collectives, body(): asked = lax.all_to_all(requests, PANEL, 0, 0, tiled=True)  35.3 us
    pallas_call x1, Pallas kernels, radiate(): pl.pallas_call(radiate_kernel, grid=(panels // PANEL_STEP,), out_shape=ja...  31 us
    all_to_all x1, blocking collectives, body(): parts = jnp.sum(lax.all_to_all(parts, SLAB, 0, 0, tiled=True), axis=0)  19 us
    all_to_all x1, blocking collectives, body(): parts = lax.all_to_all(parts.reshape(far, 1, -1), 'z', 0, 0, tiled=True)  17.2 us
    all_gather x1, blocking collectives, body(): lax.all_gather(lax.optimization_barrier((observer_points, asked))[0], 'x'...  10.8 us
    pallas_call x1, Pallas kernels, geometry(): pl.pallas_call(geometry_kernel, grid=(total // tile,), out_shape=(shape,...  8.55 us
    all_to_all x1, starting transfers between devices, body(): arrived = lax.all_to_all(found, PANEL, 0, 0, tiled=True)  6.91 us
  transfers between devices with their start and end apart: 1, of which 1 were waited for; matrix products, arithmetic and copies ran while one was open for 1% of the time, Pallas kernels for 3%

profile of v1, /device:TPU:1, one launch (start us, length us, event | category | flops | bytes accessed | tf_op | source)
XLA Modules:
  0.0 246.5 jit_solution(9271951493725982010)
XLA Ops:
  0.0 0.0 copy-start
  0.0 0.9 convert_reduce_fusion
  1.0 0.7 fusion.12
  1.6 0.8 select_reduce_fusion
  2.4 0.1 all_to_all.15
  2.5 35.3 %all_to_all.24 = s32[128,1,2]{2,1,0:T(1,128)S(1)} all-to-all(s32[128,1,2]{2,1,0:T(1,128)S(1)} %bitcast.32), channel_id=1, replica_groups=mesh['z'=16,'y'=4,'c'=2,'x'=4] {'z','y','c'}, dimensions={0} | all-to-all | bytes 2048 | tf_op jit(solution)/shard_map/all_to_all | solution.py:191
  37.8 0.5 broadcast.39
  38.3 0.8 reduce.4
  39.1 0.1 reshape.67
  39.3 0.0 copy-done
  39.3 4.2 %gather_fusion = bf16[256,4,1280]{2,1,0:T(4,128)(2,1)} fusion(bf16[128,4,1280]{2,1,0:T(4,128)(2,1)S(1)} %copy-done, s32[1024]{0:T(1024)S(1)} %pad_clamp_fusion), kind=kCustom, calls=%fused_computation | custom fusion | bytes 5243904 | tf_op jit(solution)/shard_map/gather | solution.py:192
  43.5 0.0 copy-start.3
  43.5 0.0 copy-start.4
  43.5 0.0 copy-start.1
  43.5 0.0 copy-start.2
  43.5 6.9 %all-to-all-start.1 = ((bf16[128,2,4,1280]{3,2,1,0:T(4,128)(2,1)}), bf16[128,2,4,1280]{3,2,1,0:T(4,128)(2,1)}, u32[]{:S(2)}, u32[]{:S(2)}) async-start(bf16[128,2,4,1280]{3,2,1,0:T(4,128)(2,1)} %bitcast.26), calls=%async_computation.1 | async-start | bytes 5242880 | tf_op jit(solution)/shard_map/all_to_all | solution.py:194
  50.4 0.0 copy-done.3
  50.4 0.7 copy.28
  51.1 0.0 copy-done.4
  51.1 0.7 copy.29
  51.9 0.0 copy-done.1
  51.9 0.1 copy.24
  52.0 0.2 fusion
  52.2 0.2 copy.26
  52.4 0.0 copy-done.2
  52.4 10.8 %all_gather.3.observers_ref = f32[3,1024]{1,0:T(4,128)} all-gather(f32[3,256]{1,0:T(4,128)S(1)} %copy-done.2), channel_id=1, replica_groups=mesh['z'=16,'y'=4,'c'=2,'x'=4] {'x'}, dimensions={1}, use_global_device_ids=true | all-gather | bytes 15360 | tf_op jit(solution)/shard_map/all_gather | solution.py:196
  63.3 8.5 %geometry.1 = (f32[1024,1024]{1,0:T(8,128)}, f32[1024,1024]{1,0:T(8,128)}, f32[1024,1024]{1,0:T(8,128)}) custom-call(f32[128,3]{1,0:T(8,128)} %bitcast.33, f32[3,1024]{1,0:T(4,128)} %all_gather.3.observers_ref), custom_call_target="tpu_custom_call" | custom-call | flops 26214400 | bytes 12582912 | tf_op jit(solution)/shard_map/geometry/pallas_call | solution.py:65
  71.8 0.5 cosine_multiply_fusion
  72.4 0.8 pad_maximum_fusion.table_ref
  73.1 95.6 %all-to-all-done.1 = bf16[128,2,4,1280]{3,2,1,0:T(4,128)(2,1)} async-done(((bf16[128,2,4,1280]{3,2,1,0:T(4,128)(2,1)}), bf16[128,2,4,1280]{3,2,1,0:T(4,128)(2,1)}, u32[]{:S(2)}, u32[]{:S(2)}) %all-to-all-start.1) | async-done | bytes 2621472 | tf_op jit(solution)/shard_map/all_to_all | solution.py:194
  168.8 5.3 %reshape.69 = bf16[1024,1280]{1,0:T(8,128)(2,1)} reshape(bf16[128,2,4,1280]{3,2,1,0:T(4,128)(2,1)} %all-to-all-done.1) | data formatting | bytes 5242880 | tf_op jit(solution)/shard_map/reshape | solution.py:204
  174.1 3.1 %fusion.13.values_ref = f32[128,1280]{1,0:T(8,128)} fusion(bf16[128,1024]{0,1:T(8,128)(2,1)S(1)} %bitcast.29, bf16[1024,1280]{1,0:T(8,128)(2,1)} %reshape.69), kind=kOutput, calls=%fused_computation.28 | convolution fusion | flops 335544320 | bytes 3538944 | tf_op jit(solution)/shard_map/dot_general | solution.py:204
  177.2 31.0 %radiate.1 = f32[128,1024]{1,0:T(8,128)} custom-call(f32[128,1280]{1,0:T(8,128)} %fusion.13.values_ref, f32[128,3]{1,0:T(8,128)} %bitcast.31, f32[256,128]{1,0:T(8,128)} %pad_maximum_fusion.table_ref, f32[1024,1024]{1,0:T(8,128)} %get-tuple-element.8.basis_ref, f32[1024,1024]{1,0:T(8,128)} %get-tuple-element.9.cos_ref, f32[1024,1024]{1,0:T(8,128)} %get-tuple-element.10.sin_ref), custom_call_target="tpu_custom_call" | custom-call | flops 251658240 | bytes 12582912 | tf_op jit(solution)/shard_map/radiate/pallas_call | solution.py:163
  208.2 1.3 copy.30
  209.6 19.0 %all_to_all.25 = f32[32,16,256]{2,1,0:T(8,128)S(1)} all-to-all(f32[32,16,256]{2,1,0:T(8,128)S(1)} %bitcast.27), channel_id=1, replica_groups=mesh['z'=16,'y'=4,'c'=2,'x'=4] {'y','c','x'}, dimensions={0} | all-to-all | bytes 1048576 | tf_op jit(solution)/shard_map/all_to_all | solution.py:209
  228.7 17.2 %all_to_all.26 = f32[16,1,256]{2,1,0:T(1,128)S(1)} all-to-all(f32[16,1,256]{2,1,0:T(1,128)S(1)} %reshape.72), channel_id=1, replica_groups=mesh['z'=16,'y'=4,'c'=2,'x'=4] {'z'}, dimensions={0} | all-to-all | bytes 32768 | tf_op jit(solution)/shard_map/all_to_all | solution.py:210
  245.9 0.6 reduce_sum.44
  (5 shorter events, 0.1 us)
Async XLA Ops:
  0.0 39.3 %copy-start = (bf16[128,4,1280]{2,1,0:T(4,128)(2,1)S(1)}, bf16[128,4,1280]{2,1,0:T(4,128)(2,1)}, u32[]{:S(2)}) copy-start(bf16[128,4,1280]{2,1,0:T(4,128)(2,1)} %param.7) | copy-start | bytes 3932164
  43.5 6.9 %copy-start.3 = (f32[3,128]{1,0:T(4,128)S(1)}, f32[3,128]{1,0:T(4,128)}, u32[]{:S(2)}) copy-start(f32[3,128]{1,0:T(4,128)} %param.11) | copy-start | bytes 4612
  43.5 7.7 %copy-start.4 = (f32[3,128]{1,0:T(4,128)S(1)}, f32[3,128]{1,0:T(4,128)}, u32[]{:S(2)}) copy-start(f32[3,128]{1,0:T(4,128)} %param.12) | copy-start | bytes 4612
  43.5 8.4 %copy-start.1 = (bf16[1,128,512]{2,1,0:T(8,128)(2,1)S(1)}, bf16[1,128,512]{2,1,0:T(8,128)(2,1)}, u32[]{:S(2)}) copy-start(bf16[1,128,512]{2,1,0:T(8,128)(2,1)} %param.8) | copy-start | bytes 393220
  43.5 9.0 %copy-start.2 = (f32[3,256]{1,0:T(4,128)S(1)}, f32[3,256]{1,0:T(4,128)}, u32[]{:S(2)}) copy-start(f32[3,256]{1,0:T(4,128)} %param.13) | copy-start | bytes 9220
  43.5 125.3 %all-to-all-start.1 = ((bf16[128,2,4,1280]{3,2,1,0:T(4,128)(2,1)}), bf16[128,2,4,1280]{3,2,1,0:T(4,128)(2,1)}, u32[]{:S(2)}, u32[]{:S(2)}) async-start(bf16[128,2,4,1280]{3,2,1,0:T(4,128)(2,1)} %bitcast.26), calls=%async_computation.1 | async-start | bytes 5242880 | tf_op jit(solution)/shard_map/all_to_all | solution.py:194

commit v2 on v1

v2 whole, which is shorter than its diff:
```python
import functools
import math

import jax
import jax.numpy as jnp
from jax import lax
from jax.experimental import pallas as pl
from jax.experimental.pallas import tpu as pltpu
from jax.sharding import Mesh
from jax.sharding import PartitionSpec as P

NV = 5
NT = 256
HARM = 64
KAPPA = 0.5
PANEL = ("z", "y", "c")
SLAB = ("y", "c", "x")
CAP = 2
GROUP = 8
PANEL_STEP = 32
TOGETHER = 4
OBS_TILE = 256


def harmonic_of(index):
    return (index % GROUP) * (HARM // GROUP) + index // GROUP + 1


def fourier_table(samples, orders):
    sample_ids = jnp.arange(samples, dtype=jnp.int32)
    harmonic = harmonic_of(jnp.arange(orders, dtype=jnp.int32))
    wrapped = sample_ids[:, None] * harmonic[None, :] % samples
    angles = wrapped.astype(jnp.float32) * (2.0 * math.pi / samples)
    factor = 2.0 / samples
    return jnp.concatenate([factor * jnp.cos(angles), -factor * jnp.sin(angles)], axis=1)


def geometry_kernel(points_ref, observers_ref, basis_ref, cos_ref, sin_ref):
    panels = points_ref.shape[0]
    offsets = [observers_ref[i : i + 1, :] - points_ref[:, i : i + 1] for i in range(3)]
    distance = jnp.sqrt(offsets[0] * offsets[0] + offsets[1] * offsets[1] + offsets[2] * offsets[2])
    inverse = 1.0 / distance
    weight = inverse * (1.0 / (4.0 * math.pi))
    near = weight * inverse
    rows = lambda j: pl.ds(j, panels, stride=GROUP)
    for i in range(3):
        direction = offsets[i] * inverse
        basis_ref[rows(i), :] = direction * near
        basis_ref[rows(3 + i), :] = direction * weight
    basis_ref[rows(6), :] = weight
    basis_ref[rows(7), :] = jnp.zeros_like(weight)
    phase = KAPPA * distance
    c, s = jnp.cos(phase), jnp.sin(phase)
    c8, s8 = c, s
    for _ in range(3):
        c8, s8 = c8 * c8 - s8 * s8, 2.0 * (s8 * c8)
    for j in range(GROUP):
        cos_ref[rows(j), :] = c
        sin_ref[rows(j), :] = s
        c, s = c * c8 - s * s8, s * c8 + c * s8


def geometry(points, observers):
    panels, total = points.shape[0], observers.shape[1]
    tile = 128
    shape = jax.ShapeDtypeStruct((panels * GROUP, total), jnp.float32)
    spec = pl.BlockSpec((panels * GROUP, tile), lambda x: (0, x))
    return pl.pallas_call(
        geometry_kernel,
        grid=(total // tile,),
        out_shape=(shape, shape, shape),
        in_specs=[
            pl.BlockSpec((panels, 3), lambda x: (0, 0)),
            pl.BlockSpec((3, tile), lambda x: (0, x)),
        ],
        out_specs=(spec, spec, spec),
        cost_estimate=pl.CostEstimate(
            flops=200 * panels * total, bytes_accessed=12 * panels * GROUP * total, transcendentals=3 * panels * total
        ),
        name="geometry",
    )(points, observers)


def split_two(value):
    high = value.astype(jnp.bfloat16).astype(jnp.float32)
    return high, value - high


def fill_factors(weights_ref, donors_ref, normals_ref, table_ref, factors_ref):
    slots, pairs, rows8, lanes128 = donors_ref.shape
    panels = normals_ref.shape[0]
    columns = []
    for t in range(pairs):
        block = donors_ref[:, t].reshape(slots * rows8, lanes128)
        both = jnp.dot(weights_ref[...], block, preferred_element_type=jnp.float32)
        columns += [both[:panels], both[panels:]]
    per = NT // lanes128
    field = lambda v: jnp.concatenate(columns[v * per : (v + 1) * per], axis=1)
    normal = [normals_ref[:, i : i + 1] for i in range(3)]
    flow = field(1) * normal[0] + field(2) * normal[1] + field(3) * normal[2]
    mass = (1.0 + field(0)) * flow
    loads = [field(4) * normal[i] + mass * field(1 + i) for i in range(3)]
    series = jnp.concatenate([mass] + loads, axis=0)
    spectra = jnp.dot(series, table_ref[...], precision=lax.Precision.HIGHEST, preferred_element_type=jnp.float32)
    lane = lax.broadcasted_iota(jnp.int32, (panels, 2 * HARM), 1)
    order = harmonic_of(jnp.where(lane < HARM, lane, lane - HARM)).astype(jnp.float32) * KAPPA
    wave = jnp.where(lane < HARM, -order, order)
    rows = lambda j: pl.ds(j, panels, stride=GROUP)
    for i in range(4):
        part = spectra[i * panels : (i + 1) * panels]
        turned = jnp.concatenate([part[:, HARM:], part[:, :HARM]], axis=1) * wave
        if i == 0:
            factors_ref[rows(6), :] = turned
        else:
            factors_ref[rows(i - 1), :] = part
            factors_ref[rows(2 + i), :] = turned
    factors_ref[rows(7), :] = jnp.zeros((panels, 2 * HARM), jnp.float32)


def left_factors(first, factors_ref):
    lefts = []
    for k in range(TOGETHER):
        high, low = split_two(factors_ref[pl.ds(pl.multiple_of((first + k) * GROUP, GROUP), GROUP), :])
        lefts.append(jnp.concatenate([high, high, low, jnp.zeros_like(low)], axis=0).astype(jnp.bfloat16))
    return lefts


def amplitudes(first, lefts, lanes, basis_ref, amps_ref):
    for k in range(TOGETHER):
        at = pl.multiple_of((first + k) * GROUP, GROUP)
        high, low = split_two(basis_ref[pl.ds(at, GROUP), lanes])
        right = jnp.concatenate([high, low, high, jnp.zeros_like(low)], axis=0).astype(jnp.bfloat16)
        amps_ref[k, :, lanes] = lax.dot_general(
            lefts[k], right, (((0,), (0,)), ((), ())), preferred_element_type=jnp.float32
        )


def add_up(first, lanes, amps_ref, cos_ref, sin_ref, sent_ref):
    width = sent_ref.shape[2]
    block, inner = lanes.start // width, slice(lanes.start % width, lanes.start % width + 128)
    across = cos_ref.shape[1] // width
    states = []
    for k in range(TOGETHER):
        at = pl.multiple_of((first + k) * GROUP, GROUP)
        c, s = cos_ref[pl.ds(at, GROUP), lanes], sin_ref[pl.ds(at, GROUP), lanes]
        c1 = jnp.broadcast_to(c[0:1, :], c.shape)
        s1 = jnp.broadcast_to(s[0:1, :], s.shape)
        states.append((c, s, c * c1 + s * s1, s * c1 - c * s1, 2.0 * c1))
    for r in range(HARM // GROUP):
        re = slice(r * GROUP, (r + 1) * GROUP)
        im = slice(HARM + r * GROUP, HARM + (r + 1) * GROUP)
        place = r * across + block
        total_re, total_im = sent_ref[place, 0:GROUP, inner], sent_ref[place, GROUP : 2 * GROUP, inner]
        for k in range(TOGETHER):
            c, s, before_c, before_s, twice = states[k]
            a_re, a_im = amps_ref[k, re, lanes], amps_ref[k, im, lanes]
            total_re = total_re + (a_re * c + a_im * s)
            total_im = total_im + (a_im * c - a_re * s)
            states[k] = (twice * c - before_c, twice * s - before_s, c, s, twice)
        sent_ref[place, 0:GROUP, inner] = total_re
        sent_ref[place, GROUP : 2 * GROUP, inner] = total_im


def radiate_kernel(
    weights_ref,
    donors_ref,
    normals_ref,
    table_ref,
    basis_ref,
    cos_ref,
    sin_ref,
    sent_ref,
    factors_ref,
    even_ref,
    odd_ref,
):
    step = pl.program_id(0)

    @pl.when(step == 0)
    def _():
        fill_factors(weights_ref, donors_ref, normals_ref, table_ref, factors_ref)
        sent_ref[...] = jnp.zeros_like(sent_ref)

    panel = step * PANEL_STEP
    last = PANEL_STEP - TOGETHER
    observers = basis_ref.shape[1]
    tiles = [slice(x, x + OBS_TILE) for x in range(0, observers, OBS_TILE)]
    parts = [slice(x, x + 128) for x in range(0, observers, 128)]

    lefts = left_factors(panel, factors_ref)
    for lanes in tiles:
        amplitudes(0, lefts, lanes, basis_ref, even_ref)

    def one_group(turn, carry):
        first = turn * TOGETHER
        following = jnp.minimum(first + TOGETHER, last)

        def compute(now_ref, next_ref):
            lefts = left_factors(panel + following, factors_ref)
            share = len(parts) // (len(tiles) + 1)
            done = 0
            for n, lanes in enumerate(tiles):
                for part in parts[done : done + share]:
                    add_up(first, part, now_ref, cos_ref, sin_ref, sent_ref)
                done += share
                amplitudes(following, lefts, lanes, basis_ref, next_ref)
            for part in parts[done:]:
                add_up(first, part, now_ref, cos_ref, sin_ref, sent_ref)

        pl.when(turn % 2 == 0)(lambda: compute(even_ref, odd_ref))
        pl.when(turn % 2 == 1)(lambda: compute(odd_ref, even_ref))
        return carry

    lax.fori_loop(0, PANEL_STEP // TOGETHER, one_group, 0)


def radiate(weights, donors, normals, table, basis, cosines, sines, sent):
    panels, observers = normals.shape[0], basis.shape[1]
    whole = lambda a: pl.BlockSpec(a.shape, lambda p: (0,) * len(a.shape))
    rows = pl.BlockSpec((PANEL_STEP * GROUP, observers), lambda p: (p, 0))
    return pl.pallas_call(
        radiate_kernel,
        grid=(panels // PANEL_STEP,),
        out_shape=sent,
        in_specs=[whole(weights), whole(donors), whole(normals), whole(table), rows, rows, rows],
        out_specs=whole(sent),
        scratch_shapes=[
            pltpu.VMEM((panels * GROUP, 2 * HARM), jnp.float32),
            pltpu.VMEM((TOGETHER, 2 * HARM, observers), jnp.float32),
            pltpu.VMEM((TOGETHER, 2 * HARM, observers), jnp.float32),
        ],
        cost_estimate=pl.CostEstimate(
            flops=30 * panels * HARM * observers, bytes_accessed=12 * panels * GROUP * observers, transcendentals=0
        ),
        name="radiate",
    )(weights, donors, normals, table, basis, cosines, sines)


def gather_kernel(asked_ref, blocks_ref, found_ref):
    peers = found_ref.shape[0]
    first = pl.program_id(0) * peers
    for i in range(peers):
        word = asked_ref[first + i]
        found_ref[i, 0] = blocks_ref[word & 0xFFFF]
        found_ref[i, 1] = blocks_ref[word >> 16]


def gather(asked, blocks):
    peers, together = asked.shape[0], 16
    rest = blocks.shape[1:]
    return pl.pallas_call(
        gather_kernel,
        grid_spec=pltpu.PrefetchScalarGridSpec(
            num_scalar_prefetch=1,
            grid=(peers // together,),
            in_specs=[pl.BlockSpec(blocks.shape, lambda p, asked: (0, 0, 0, 0))],
            out_specs=pl.BlockSpec((together, CAP) + rest, lambda p, asked: (p, 0, 0, 0, 0)),
        ),
        out_shape=jax.ShapeDtypeStruct((peers, CAP) + rest, blocks.dtype),
        name="gather",
    )(asked, blocks)


def body(flow_blocks, interp_weights, donor_owner, donor_block, panel_normals, panel_points, observer_points):
    peers = lax.axis_size(PANEL)
    cells, history = flow_blocks.shape[1:]
    width = interp_weights.shape[1]
    slots = donor_block.shape[0]
    owner = donor_owner[:, 0]

    row = jnp.arange(slots, dtype=jnp.int32)
    same = (owner[:, None] == owner[None, :]) & (row[None, :] < row[:, None])
    rank = jnp.sum(same.astype(jnp.int32), axis=1)
    slot = owner * CAP + rank
    slot_ids = jnp.arange(peers * CAP, dtype=jnp.int32)
    chosen = slot[:, None] == slot_ids[None, :]
    held = flow_blocks.shape[0]
    word = jnp.where(rank == 0, donor_block, donor_block << 16)
    named = owner[:, None] == jnp.arange(peers, dtype=jnp.int32)[None, :]
    requests = jnp.sum(jnp.where(named, word[:, None], 0), axis=0)
    asked = lax.all_to_all(requests, PANEL, 0, 0, tiled=True)
    tiles = history // 256
    blocks = flow_blocks.reshape(held, cells, tiles, 2, 128).transpose(0, 2, 3, 1, 4).reshape(held, tiles, 2 * cells, 128)
    arrived = lax.all_to_all(gather(asked, blocks), PANEL, 0, 0, tiled=True).reshape(peers * CAP, tiles, 2 * cells, 128)

    observers = lax.all_gather(lax.optimization_barrier((observer_points, asked))[0], "x", axis=1, tiled=True)
    basis, cosines, sines = geometry(panel_points.T, observers)
    table = fourier_table(NT, HARM)
    placing = chosen.astype(jnp.bfloat16)
    weights = interp_weights.reshape(width, slots, cells)
    placed = jnp.einsum("prc,rs->psc", weights, placing, preferred_element_type=jnp.float32).astype(jnp.bfloat16)
    halves = jnp.eye(2, dtype=jnp.bfloat16)[:, None, None, :, None] * placed[None, :, :, None, :]
    halves = halves.reshape(2 * width, peers * CAP * 2 * cells)

    far, near, across = lax.axis_size("z"), lax.axis_size(("y", "c")), lax.axis_size("x")
    sent = jax.ShapeDtypeStruct((near * across, far, observer_points.shape[1]), jnp.float32)
    parts = radiate(halves, arrived, panel_normals.T, table, basis, cosines, sines, sent)
    parts = jnp.sum(lax.all_to_all(parts, SLAB, 0, 0, tiled=True), axis=0)
    parts = lax.all_to_all(parts.reshape(far, 1, -1), "z", 0, 0, tiled=True)
    return jnp.sum(parts, axis=0)


def solution(mesh):
    panel, obs = mesh.shape["panel"], mesh.shape["obs"]
    finer = Mesh(mesh.devices.reshape(panel // 8, 4, 2, obs), ("z", "y", "c", "x"))
    every = PANEL + ("x",)
    in_specs = (
        P(PANEL, None, None),
        P(every, None, None),
        P(every, None),
        P(every),
        P(None, every),
        P(None, every),
        P(None, "x"),
    )
    return jax.shard_map(body, mesh=finer, in_specs=in_specs, out_specs=P(PANEL, "x"), check_vma=False)
```

time: 247 us -> 238 us (0.964)
  local copies, waits for them, and re-layouts: 13.4 us -> 6.81 us
  waiting for transfers between devices: 95.6 us -> 91.7 us
  matrix products: 3.37 us -> 0.22 us
  Pallas kernels: 39.5 us -> 42.5 us
  other arithmetic: 5.13 us -> 8.07 us
    reshape x3 -> x0, local copies, waits for them, and re-layouts: 6.8 us -> none  [the longest x1 5.32 us: body(): arrived.reshape(-1, history)]
    gather x1 -> x0, local copies, waits for them, and re-layouts: 4.17 us -> none  [body(): found = flow_blocks.at[asked.reshape(-1)].get(mode='promise_in_bounds')]
    all_to_all x1, waiting for transfers between devices: 95.6 us -> 91.7 us  [body(): lax.all_to_all(gather(asked, blocks), PANEL, 0, 0, tiled=True)]
    dot_general x1 -> x0, matrix products: 3.15 us -> none  [body(): jnp.dot(placed, arrived.reshape(-1, history), preferred_element_type=jnp....]
    pallas_call x1 -> x2, Pallas kernels: 31 us -> 33.7 us  [the longest x1 28.4 us: radiate(): pl.pallas_call(radiate_kernel, grid=(panels // PANEL_STEP,), out_shape=se...]
    unnamed x13 -> x16, local copies, waits for them, and re-layouts: 1.59 us -> 4.21 us
  transfers between devices with their start and end apart: 1 -> 1, of which waited for: 1 -> 1; matrix products, arithmetic and copies ran while one was open for 1% -> 3% of each run, Pallas kernels for 3% -> 4%
where the time goes in v2:
time: 238 us; the launch traced here: 237 us
  waiting for transfers between devices  91.7 us (39%)
  blocking collectives  82.2 us (35%)
  Pallas kernels  42.5 us (18%)
  other arithmetic  8.07 us (3%)
  local copies, waits for them, and re-layouts  6.81 us (3%)
  starting transfers between devices  5.77 us (2%)
    all_to_all x1, waiting for transfers between devices, body(): lax.all_to_all(gather(asked, blocks), PANEL, 0, 0, tiled=True)  91.7 us
    all_to_all x1, blocking collectives, body(): asked = lax.all_to_all(requests, PANEL, 0, 0, tiled=True)  35.3 us
    pallas_call x1, Pallas kernels, radiate(): pl.pallas_call(radiate_kernel, grid=(panels // PANEL_STEP,), out_shape=se...  28.4 us
    all_to_all x1, blocking collectives, body(): parts = jnp.sum(lax.all_to_all(parts, SLAB, 0, 0, tiled=True), axis=0)  19.2 us
    all_to_all x1, blocking collectives, body(): parts = lax.all_to_all(parts.reshape(far, 1, -1), 'z', 0, 0, tiled=True)  17.2 us
    all_gather x1, blocking collectives, body(): lax.all_gather(lax.optimization_barrier((observer_points, asked))[0], 'x'...  10.5 us
    pallas_call x1, Pallas kernels, geometry(): pl.pallas_call(geometry_kernel, grid=(total // tile,), out_shape=(shape,...  8.73 us
    all_to_all x1, starting transfers between devices, body(): lax.all_to_all(gather(asked, blocks), PANEL, 0, 0, tiled=True)  5.77 us
  transfers between devices with their start and end apart: 1, of which 1 were waited for; matrix products, arithmetic and copies ran while one was open for 3% of the time, Pallas kernels for 4%

profile of v2, /device:TPU:1, one launch (start us, length us, event | category | flops | bytes accessed | tf_op | source)
XLA Modules:
  0.0 237.3 jit_solution(6476511341759353600)
XLA Ops:
  0.0 0.9 convert_reduce_fusion
  0.9 0.7 compare_select_fusion
  1.6 0.8 select_reduce_fusion
  2.3 0.1 copy.39
  2.5 35.3 %all_to_all.26 = s32[128,1,1]{2,1,0:T(1,128)S(1)} all-to-all(s32[128,1,1]{2,1,0:T(1,128)S(1)} %copy.39), channel_id=1, replica_groups=mesh['z'=16,'y'=4,'c'=2,'x'=4] {'z','y','c'}, dimensions={0} | all-to-all | bytes 1024 | tf_op jit(solution)/shard_map/all_to_all | solution.py:281
  37.7 2.9 %reduce.1.asked_ref = s32[128]{0:T(128)} reduce(s32[128,1,1]{2,1,0:T(1,128)S(1)} %all_to_all.26, s32[]{:T(128)} %constant.48.clone.1), dimensions={1,2}, to_apply=%all_to_all.17.reduce_sub_computation | reduce | bytes 1028 | tf_op jit(solution)/shard_map/all_to_all | solution.py:281
  40.6 0.0 copy-start.3
  40.6 0.0 copy-start.4
  40.6 0.0 copy-start.1
  40.6 0.0 copy-start.5
  40.6 5.4 %gather.1 = bf16[128,2,5,8,128]{4,3,2,1,0:T(8,128)(2,1)} custom-call(s32[128]{0:T(128)} %reduce.1.asked_ref, bf16[128,5,8,128]{3,2,1,0:T(8,128)(2,1)} %bitcast.33), custom_call_target="tpu_custom_call" | custom-call | tf_op jit(solution)/shard_map/gather/pallas_call | solution.py:251
  46.0 5.8 %all-to-all-start.1 = ((bf16[128,2,5,8,128]{4,3,2,1,0:T(8,128)(2,1)}), bf16[128,2,5,8,128]{4,3,2,1,0:T(8,128)(2,1)S(1)}, u32[]{:S(2)}, u32[]{:S(2)}) async-start(bf16[128,2,5,8,128]{4,3,2,1,0:T(8,128)(2,1)} %gather.1), calls=%async_computation.1 | async-start | bytes 5242880 | tf_op jit(solution)/shard_map/all_to_all | solution.py:284
  51.7 0.0 copy-done.3
  51.8 0.0 copy-start.2
  51.8 0.7 copy.41
  52.5 0.0 copy-done.4
  52.5 0.7 copy.42
  53.2 0.0 copy-done.1
  53.2 0.1 copy.36
  53.4 0.0 copy-done.5
  53.4 0.2 fusion
  53.6 0.2 copy.38
  53.8 0.9 broadcast_multiply_fusion
  54.8 1.1 copy.48
  55.9 2.3 copy.43.weights_ref
  58.2 0.5 cosine_multiply_fusion
  58.7 0.7 pad_maximum_fusion.table_ref
  59.4 0.0 copy-done.2
  59.4 10.5 %all_gather.3.observers_ref = f32[3,1024]{1,0:T(4,128)} all-gather(f32[3,256]{1,0:T(4,128)S(1)} %copy-done.2), channel_id=1, replica_groups=mesh['z'=16,'y'=4,'c'=2,'x'=4] {'x'}, dimensions={1}, use_global_device_ids=true | all-gather | bytes 15360 | tf_op jit(solution)/shard_map/all_gather | solution.py:286
  70.0 8.7 %geometry.1 = (f32[1024,1024]{1,0:T(8,128)}, f32[1024,1024]{1,0:T(8,128)}, f32[1024,1024]{1,0:T(8,128)}) custom-call(f32[128,3]{1,0:T(8,128)} %bitcast.36, f32[3,1024]{1,0:T(4,128)} %all_gather.3.observers_ref), custom_call_target="tpu_custom_call" | custom-call | flops 26214400 | bytes 12582912 | tf_op jit(solution)/shard_map/geometry/pallas_call | solution.py:68
  78.7 91.7 %all-to-all-done.1 = bf16[128,2,5,8,128]{4,3,2,1,0:T(8,128)(2,1)S(1)} async-done(((bf16[128,2,5,8,128]{4,3,2,1,0:T(8,128)(2,1)}), bf16[128,2,5,8,128]{4,3,2,1,0:T(8,128)(2,1)S(1)}, u32[]{:S(2)}, u32[]{:S(2)}) %all-to-all-start.1) | async-done | bytes 2621472 | tf_op jit(solution)/shard_map/all_to_all | solution.py:284
  170.4 0.0 copy-start
  170.4 1.5 copy-done
  171.9 28.4 %radiate.1 = f32[32,16,256]{2,1,0:T(8,128)} custom-call(bf16[256,2048]{1,0:T(8,128)(2,1)} %copy.43.weights_ref, bf16[256,5,8,128]{3,2,1,0:T(8,128)(2,1)} %bitcast.30, f32[128,3]{1,0:T(8,128)} %bitcast.35, f32[256,128]{1,0:T(8,128)} %pad_maximum_fusion.table_ref, f32[1024,1024]{1,0:T(8,128)} %get-tuple-element.10.basis_ref, ...), custom_call_target="tpu_custom_call" | custom-call | flops 251658240 | bytes 12582912 | tf_op jit(solution)/shard_map/radiate/pallas_call | solution.py:221
  200.3 19.2 %all_to_all.27 = f32[32,16,256]{2,1,0:T(8,128)S(1)} all-to-all(f32[32,16,256]{2,1,0:T(8,128)} %radiate.1), channel_id=1, replica_groups=mesh['z'=16,'y'=4,'c'=2,'x'=4] {'y','c','x'}, dimensions={0} | all-to-all | bytes 1048576 | tf_op jit(solution)/shard_map/all_to_all | solution.py:298
  219.5 17.2 %all_to_all.28 = f32[16,1,256]{2,1,0:T(1,128)S(1)} all-to-all(f32[16,1,256]{2,1,0:T(1,128)S(1)} %reshape.61), channel_id=1, replica_groups=mesh['z'=16,'y'=4,'c'=2,'x'=4] {'z'}, dimensions={0} | all-to-all | bytes 32768 | tf_op jit(solution)/shard_map/all_to_all | solution.py:299
  236.7 0.6 reduce_sum.44
  (5 shorter events, 0.1 us)
Async XLA Ops:
  40.6 11.2 %copy-start.3 = (f32[3,128]{1,0:T(4,128)S(1)}, f32[3,128]{1,0:T(4,128)}, u32[]{:S(2)}) copy-start(f32[3,128]{1,0:T(4,128)} %param.11) | copy-start | bytes 4612
  40.6 11.9 %copy-start.4 = (f32[3,128]{1,0:T(4,128)S(1)}, f32[3,128]{1,0:T(4,128)}, u32[]{:S(2)}) copy-start(f32[3,128]{1,0:T(4,128)} %param.12) | copy-start | bytes 4612
  40.6 12.7 %copy-start.1 = (bf16[1,128,512]{2,1,0:T(8,128)(2,1)S(1)}, bf16[1,128,512]{2,1,0:T(8,128)(2,1)}, u32[]{:S(2)}) copy-start(bf16[1,128,512]{2,1,0:T(8,128)(2,1)} %param.8) | copy-start | bytes 393220
  40.6 12.8 %copy-start.5 = (s32[128,1]{0,1:T(1,128)S(1)}, s32[128,1]{0,1:T(1,128)}, u32[]{:S(2)}) copy-start(s32[128,1]{0,1:T(1,128)} %param.9) | copy-start | bytes 1540
  46.0 124.5 %all-to-all-start.1 = ((bf16[128,2,5,8,128]{4,3,2,1,0:T(8,128)(2,1)}), bf16[128,2,5,8,128]{4,3,2,1,0:T(8,128)(2,1)S(1)}, u32[]{:S(2)}, u32[]{:S(2)}) async-start(bf16[128,2,5,8,128]{4,3,2,1,0:T(8,128)(2,1)} %gather.1), calls=%async_computation.1 | async-start | bytes 5242880 | tf_op jit(solution)/shard_map/all_to_all | solution.py:284
  51.8 7.7 %copy-start.2 = (f32[3,256]{1,0:T(4,128)S(1)}, f32[3,256]{1,0:T(4,128)}, u32[]{:S(2)}) copy-start(f32[3,256]{1,0:T(4,128)} %param.13) | copy-start | bytes 9220
  170.4 1.5 copy-start

commit v3 on v2

--- a/solution.py
+++ b/solution.py
@@ -35,7 +35,8 @@
     return jnp.concatenate([factor * jnp.cos(angles), -factor * jnp.sin(angles)], axis=1)
 
 
-def geometry_kernel(points_ref, observers_ref, basis_ref, cos_ref, sin_ref):
+def geometry_kernel(points_ref, observers_ref, made_ref):
+    basis_ref, cos_ref, sin_ref = (made_ref.at[n] for n in range(3))
     panels = points_ref.shape[0]
     offsets = [observers_ref[i : i + 1, :] - points_ref[:, i : i + 1] for i in range(3)]
     distance = jnp.sqrt(offsets[0] * offsets[0] + offsets[1] * offsets[1] + offsets[2] * offsets[2])
@@ -63,17 +64,15 @@
 def geometry(points, observers):
     panels, total = points.shape[0], observers.shape[1]
     tile = 128
-    shape = jax.ShapeDtypeStruct((panels * GROUP, total), jnp.float32)
-    spec = pl.BlockSpec((panels * GROUP, tile), lambda x: (0, x))
     return pl.pallas_call(
         geometry_kernel,
         grid=(total // tile,),
-        out_shape=(shape, shape, shape),
+        out_shape=jax.ShapeDtypeStruct((3, panels * GROUP, total), jnp.float32),
         in_specs=[
             pl.BlockSpec((panels, 3), lambda x: (0, 0)),
             pl.BlockSpec((3, tile), lambda x: (0, x)),
         ],
-        out_specs=(spec, spec, spec),
+        out_specs=pl.BlockSpec((3, panels * GROUP, tile), lambda x: (0, 0, x)),
         cost_estimate=pl.CostEstimate(
             flops=200 * panels * total, bytes_accessed=12 * panels * GROUP * total, transcendentals=3 * panels * total
         ),
@@ -166,40 +165,51 @@
     donors_ref,
     normals_ref,
     table_ref,
-    basis_ref,
-    cos_ref,
-    sin_ref,
+    made_hbm,
     sent_ref,
+    made_ref,
     factors_ref,
     even_ref,
     odd_ref,
+    arrived,
 ):
-    step = pl.program_id(0)
-
-    @pl.when(step == 0)
-    def _():
-        fill_factors(weights_ref, donors_ref, normals_ref, table_ref, factors_ref)
-        sent_ref[...] = jnp.zeros_like(sent_ref)
-
-    panel = step * PANEL_STEP
-    last = PANEL_STEP - TOGETHER
+    size = PANEL_STEP * GROUP
+    basis_ref, cos_ref, sin_ref = (made_ref.at[n] for n in range(3))
+
+    def fetch(chunk):
+        rows = pl.ds(pl.multiple_of(chunk * size, size), size)
+        return pltpu.make_async_copy(made_hbm.at[:, rows, :], made_ref.at[:, rows, :], arrived.at[chunk])
+
+    panels = normals_ref.shape[0]
+    for chunk in range(panels // PANEL_STEP):
+        fetch(chunk).start()
+    fill_factors(weights_ref, donors_ref, normals_ref, table_ref, factors_ref)
+    sent_ref[...] = jnp.zeros_like(sent_ref)
+    fetch(0).wait()
+
+    last = panels - TOGETHER
     observers = basis_ref.shape[1]
     tiles = [slice(x, x + OBS_TILE) for x in range(0, observers, OBS_TILE)]
     parts = [slice(x, x + 128) for x in range(0, observers, 128)]
 
-    lefts = left_factors(panel, factors_ref)
+    lefts = left_factors(0, factors_ref)
     for lanes in tiles:
         amplitudes(0, lefts, lanes, basis_ref, even_ref)
 
     def one_group(turn, carry):
         first = turn * TOGETHER
         following = jnp.minimum(first + TOGETHER, last)
+        due = (first + TOGETHER) // PANEL_STEP
+
+        @pl.when(((first + TOGETHER) % PANEL_STEP == 0) & (first < last))
+        def _():
+            fetch(due).wait()
 
         def compute(now_ref, next_ref):
-            lefts = left_factors(panel + following, factors_ref)
+            lefts = left_factors(following, factors_ref)
             share = len(parts) // (len(tiles) + 1)
             done = 0
-            for n, lanes in enumerate(tiles):
+            for lanes in tiles:
                 for part in parts[done : done + share]:
                     add_up(first, part, now_ref, cos_ref, sin_ref, sent_ref)
                 done += share
@@ -211,52 +221,53 @@
         pl.when(turn % 2 == 1)(lambda: compute(odd_ref, even_ref))
         return carry
 
-    lax.fori_loop(0, PANEL_STEP // TOGETHER, one_group, 0)
-
-
-def radiate(weights, donors, normals, table, basis, cosines, sines, sent):
-    panels, observers = normals.shape[0], basis.shape[1]
-    whole = lambda a: pl.BlockSpec(a.shape, lambda p: (0,) * len(a.shape))
-    rows = pl.BlockSpec((PANEL_STEP * GROUP, observers), lambda p: (p, 0))
+    lax.fori_loop(0, panels // TOGETHER, one_group, 0)
+
+
+def radiate(weights, donors, normals, table, made, sent):
+    panels, observers = normals.shape[0], made.shape[2]
+    near, far = pl.BlockSpec(memory_space=pltpu.VMEM), pl.BlockSpec(memory_space=pltpu.HBM)
+    amps = pltpu.VMEM((TOGETHER, 2 * HARM, observers), jnp.float32)
     return pl.pallas_call(
         radiate_kernel,
-        grid=(panels // PANEL_STEP,),
         out_shape=sent,
-        in_specs=[whole(weights), whole(donors), whole(normals), whole(table), rows, rows, rows],
-        out_specs=whole(sent),
+        in_specs=[near, near, near, near, far],
+        out_specs=near,
         scratch_shapes=[
+            pltpu.VMEM(made.shape, jnp.float32),
             pltpu.VMEM((panels * GROUP, 2 * HARM), jnp.float32),
-            pltpu.VMEM((TOGETHER, 2 * HARM, observers), jnp.float32),
-            pltpu.VMEM((TOGETHER, 2 * HARM, observers), jnp.float32),
+            amps,
+            amps,
+            pltpu.SemaphoreType.DMA((panels // PANEL_STEP,)),
         ],
+        compiler_params=pltpu.CompilerParams(vmem_limit_bytes=46 * 2**20),
         cost_estimate=pl.CostEstimate(
             flops=30 * panels * HARM * observers, bytes_accessed=12 * panels * GROUP * observers, transcendentals=0
         ),
         name="radiate",
-    )(weights, donors, normals, table, basis, cosines, sines)
-
-
-def gather_kernel(asked_ref, blocks_ref, found_ref):
+    )(weights, donors, normals, table, made)
+
+
+def gather_kernel(asked_ref, blocks_ref, found_ref, sent):
     peers = found_ref.shape[0]
-    first = pl.program_id(0) * peers
-    for i in range(peers):
-        word = asked_ref[first + i]
-        found_ref[i, 0] = blocks_ref[word & 0xFFFF]
-        found_ref[i, 1] = blocks_ref[word >> 16]
+
+    def one_peer(peer, carry):
+        word = asked_ref[peer, 0, 0]
+        pltpu.make_async_copy(blocks_ref.at[word & 0xFFFF], found_ref.at[peer, 0], sent).start()
+        pltpu.make_async_copy(blocks_ref.at[word >> 16], found_ref.at[peer, 1], sent).start()
+        return carry
+
+    lax.fori_loop(0, peers, one_peer, 0, unroll=8)
+    pltpu.make_async_copy(found_ref, found_ref, sent).wait()
 
 
 def gather(asked, blocks):
-    peers, together = asked.shape[0], 16
-    rest = blocks.shape[1:]
     return pl.pallas_call(
         gather_kernel,
-        grid_spec=pltpu.PrefetchScalarGridSpec(
-            num_scalar_prefetch=1,
-            grid=(peers // together,),
-            in_specs=[pl.BlockSpec(blocks.shape, lambda p, asked: (0, 0, 0, 0))],
-            out_specs=pl.BlockSpec((together, CAP) + rest, lambda p, asked: (p, 0, 0, 0, 0)),
-        ),
-        out_shape=jax.ShapeDtypeStruct((peers, CAP) + rest, blocks.dtype),
+        in_specs=[pl.BlockSpec(memory_space=pltpu.SMEM), pl.BlockSpec(memory_space=pltpu.VMEM)],
+        out_specs=pl.BlockSpec(memory_space=pltpu.HBM),
+        out_shape=jax.ShapeDtypeStruct((asked.shape[0], CAP) + blocks.shape[1:], blocks.dtype),
+        scratch_shapes=[pltpu.SemaphoreType.DMA],
         name="gather",
     )(asked, blocks)
 
@@ -268,24 +279,24 @@
     slots = donor_block.shape[0]
     owner = donor_owner[:, 0]
 
-    row = jnp.arange(slots, dtype=jnp.int32)
-    same = (owner[:, None] == owner[None, :]) & (row[None, :] < row[:, None])
-    rank = jnp.sum(same.astype(jnp.int32), axis=1)
-    slot = owner * CAP + rank
-    slot_ids = jnp.arange(peers * CAP, dtype=jnp.int32)
-    chosen = slot[:, None] == slot_ids[None, :]
     held = flow_blocks.shape[0]
-    word = jnp.where(rank == 0, donor_block, donor_block << 16)
     named = owner[:, None] == jnp.arange(peers, dtype=jnp.int32)[None, :]
-    requests = jnp.sum(jnp.where(named, word[:, None], 0), axis=0)
-    asked = lax.all_to_all(requests, PANEL, 0, 0, tiled=True)
+    lower = jnp.min(jnp.where(named, donor_block[:, None], held), axis=0)
+    higher = jnp.max(jnp.where(named, donor_block[:, None], 0), axis=0)
+    requests = jnp.where(lower == held, 0, lower) + (higher << 16)
+    requests = lax.optimization_barrier(requests)
+    asked = lax.all_to_all(requests.reshape(peers, 1, 1), PANEL, 0, 0, tiled=True)
     tiles = history // 256
     blocks = flow_blocks.reshape(held, cells, tiles, 2, 128).transpose(0, 2, 3, 1, 4).reshape(held, tiles, 2 * cells, 128)
     arrived = lax.all_to_all(gather(asked, blocks), PANEL, 0, 0, tiled=True).reshape(peers * CAP, tiles, 2 * cells, 128)
 
     observers = lax.all_gather(lax.optimization_barrier((observer_points, asked))[0], "x", axis=1, tiled=True)
-    basis, cosines, sines = geometry(panel_points.T, observers)
+    made = geometry(panel_points.T, observers)
     table = fourier_table(NT, HARM)
+    row = jnp.arange(slots, dtype=jnp.int32)
+    key = donor_block * slots + row
+    rank = jnp.sum(((owner[:, None] == owner[None, :]) & (key[None, :] < key[:, None])).astype(jnp.int32), axis=1)
+    chosen = (owner * CAP + rank)[:, None] == jnp.arange(peers * CAP, dtype=jnp.int32)[None, :]
     placing = chosen.astype(jnp.bfloat16)
     weights = interp_weights.reshape(width, slots, cells)
     placed = jnp.einsum("prc,rs->psc", weights, placing, preferred_element_type=jnp.float32).astype(jnp.bfloat16)
@@ -294,7 +305,7 @@
 
     far, near, across = lax.axis_size("z"), lax.axis_size(("y", "c")), lax.axis_size("x")
     sent = jax.ShapeDtypeStruct((near * across, far, observer_points.shape[1]), jnp.float32)
-    parts = radiate(halves, arrived, panel_normals.T, table, basis, cosines, sines, sent)
+    parts = radiate(halves, arrived, panel_normals.T, table, made, sent)
     parts = jnp.sum(lax.all_to_all(parts, SLAB, 0, 0, tiled=True), axis=0)
     parts = lax.all_to_all(parts.reshape(far, 1, -1), "z", 0, 0, tiled=True)
     return jnp.sum(parts, axis=0)

time: 238 us -> 227 us (0.954)
  Pallas kernels: 42.5 us -> 35.9 us
  other arithmetic: 8.07 us -> 3.8 us
    pallas_call x3, Pallas kernels: 42.5 us -> 35.9 us  [the longest x1 23.6 us: radiate(): pl.pallas_call(radiate_kernel, out_shape=sent, in_specs=[near, near, near...]
    all_to_all x1 -> x0, other arithmetic: 2.87 us -> none  [body(): asked = lax.all_to_all(requests, PANEL, 0, 0, tiled=True)]
where the time goes in v3:
time: 227 us
  waiting for transfers between devices  92.9 us (41%)
  blocking collectives  81.9 us (36%)
  Pallas kernels  35.9 us (16%)
  local copies, waits for them, and re-layouts  5.94 us (3%)
  starting transfers between devices  5.75 us (3%)
  other arithmetic  3.8 us (2%)
    all_to_all x1, waiting for transfers between devices, body(): lax.all_to_all(gather(asked, blocks), PANEL, 0, 0, tiled=True)  92.9 us
    all_to_all x1, blocking collectives, body(): lax.all_to_all(requests.reshape(peers, 1, 1), PANEL, 0, 0, tiled=True)  35.4 us
    pallas_call x1, Pallas kernels, radiate(): pl.pallas_call(radiate_kernel, out_shape=sent, in_specs=[near, near, near...  23.6 us
    all_to_all x1, blocking collectives, body(): parts = jnp.sum(lax.all_to_all(parts, SLAB, 0, 0, tiled=True), axis=0)  19 us
    all_to_all x1, blocking collectives, body(): parts = lax.all_to_all(parts.reshape(far, 1, -1), 'z', 0, 0, tiled=True)  17.2 us
    all_gather x1, blocking collectives, body(): lax.all_gather(lax.optimization_barrier((observer_points, asked))[0], 'x'...  10.4 us
    pallas_call x1, Pallas kernels, geometry(): pl.pallas_call(geometry_kernel, grid=(total // tile,), out_shape=jax.Shap...  8.94 us
    all_to_all x1, starting transfers between devices, body(): lax.all_to_all(gather(asked, blocks), PANEL, 0, 0, tiled=True)  5.75 us
  transfers between devices with their start and end apart: 1, of which 1 were waited for; matrix products, arithmetic and copies ran while one was open for 3% of the time, Pallas kernels for 4%

profile of v3, /device:TPU:1, one launch (start us, length us, event | category | flops | bytes accessed | tf_op | source)
XLA Modules:
  0.0 226.6 jit_solution(16173795057838213678)
XLA Ops:
  0.0 0.7 iota_add_fusion
  0.7 0.9 select_reduce_fusion
  1.6 0.1 copy.33
  1.7 35.4 %all_to_all.20.asked_ref = s32[128,1,1]{2,1,0:T(1,128)} all-to-all(s32[128,1,1]{2,1,0:T(1,128)S(1)} %copy.33), channel_id=1, replica_groups=mesh['z'=16,'y'=4,'c'=2,'x'=4] {'z','y','c'}, dimensions={0} | all-to-all | bytes 1024 | tf_op jit(solution)/shard_map/all_to_all | solution.py:288
  37.0 3.4 %gather.1 = bf16[128,2,5,8,128]{4,3,2,1,0:T(8,128)(2,1)} custom-call(s32[128,1,1]{2,1,0:T(1,128)} %all_to_all.20.asked_ref, bf16[128,5,8,128]{3,2,1,0:T(8,128)(2,1)} %bitcast.34), custom_call_target="tpu_custom_call" | custom-call | tf_op jit(solution)/shard_map/gather/pallas_call | solution.py:265
  40.5 0.0 copy-start.3
  40.5 0.0 copy-start.4
  40.5 0.0 copy-start.1
  40.5 0.0 copy-start.5
  40.5 5.7 %all-to-all-start.1 = ((bf16[128,2,5,8,128]{4,3,2,1,0:T(8,128)(2,1)}), bf16[128,2,5,8,128]{4,3,2,1,0:T(8,128)(2,1)S(1)}, u32[]{:S(2)}, u32[]{:S(2)}) async-start(bf16[128,2,5,8,128]{4,3,2,1,0:T(8,128)(2,1)} %gather.1), calls=%async_computation.1 | async-start | bytes 5242880 | tf_op jit(solution)/shard_map/all_to_all | solution.py:291
  46.3 0.0 copy-done.3
  46.3 0.1 copy.35
  46.4 0.0 copy-done.4
  46.4 0.7 copy.36
  47.1 0.0 copy-done.1
  47.1 0.1 copy.30
  47.3 0.0 copy-done.5
  47.3 0.2 fusion
  47.5 0.2 copy.32
  47.7 0.9 broadcast_multiply_fusion
  48.7 0.0 copy-start.2
  48.7 1.1 copy.42
  49.8 2.3 copy.37.weights_ref
  52.1 0.5 cosine_multiply_fusion
  52.6 0.1 pad_maximum_fusion.table_ref
  52.7 0.0 copy-done.2
  52.7 10.4 %all_gather.3.observers_ref = f32[3,1024]{1,0:T(4,128)} all-gather(f32[3,256]{1,0:T(4,128)S(1)} %copy-done.2), channel_id=1, replica_groups=mesh['z'=16,'y'=4,'c'=2,'x'=4] {'x'}, dimensions={1}, use_global_device_ids=true | all-gather | bytes 15360 | tf_op jit(solution)/shard_map/all_gather | solution.py:293
  63.1 8.9 %geometry.1.made_hbm = f32[3,1024,1024]{2,1,0:T(8,128)} custom-call(f32[128,3]{1,0:T(8,128)} %bitcast.36, f32[3,1024]{1,0:T(4,128)} %all_gather.3.observers_ref), custom_call_target="tpu_custom_call" | custom-call | flops 26214400 | bytes 12582912 | tf_op jit(solution)/shard_map/geometry/pallas_call | solution.py:67
  72.1 92.9 %all-to-all-done.1 = bf16[128,2,5,8,128]{4,3,2,1,0:T(8,128)(2,1)S(1)} async-done(((bf16[128,2,5,8,128]{4,3,2,1,0:T(8,128)(2,1)}), bf16[128,2,5,8,128]{4,3,2,1,0:T(8,128)(2,1)S(1)}, u32[]{:S(2)}, u32[]{:S(2)}) %all-to-all-start.1) | async-done | bytes 2621472 | tf_op jit(solution)/shard_map/all_to_all | solution.py:291
  164.9 0.0 copy-start
  165.0 1.2 copy-done
  166.2 23.6 %radiate.1 = f32[32,16,256]{2,1,0:T(8,128)S(1)} custom-call(bf16[256,2048]{1,0:T(8,128)(2,1)S(1)} %copy-done, bf16[256,5,8,128]{3,2,1,0:T(8,128)(2,1)S(1)} %bitcast.30, f32[128,3]{1,0:T(8,128)S(1)} %bitcast.31, f32[256,128]{1,0:T(8,128)S(1)} %pad_maximum_fusion.table_ref, f32[3,1024,1024]{2,1,0:T(8,128)} %geometry.1.made_hbm), custom_call_target="tpu_custom_call" | custom-call | flops 251658240 | bytes 12582912 | tf_op jit(solution)/shard_map/radiate/pallas_call | solution.py:231
  189.8 19.0 %all_to_all.21 = f32[32,16,256]{2,1,0:T(8,128)S(1)} all-to-all(f32[32,16,256]{2,1,0:T(8,128)S(1)} %radiate.1), channel_id=1, replica_groups=mesh['z'=16,'y'=4,'c'=2,'x'=4] {'y','c','x'}, dimensions={0} | all-to-all | bytes 1048576 | tf_op jit(solution)/shard_map/all_to_all | solution.py:309
  208.8 17.2 %all_to_all.22 = f32[16,1,256]{2,1,0:T(1,128)S(1)} all-to-all(f32[16,1,256]{2,1,0:T(1,128)S(1)} %reshape.65), channel_id=1, replica_groups=mesh['z'=16,'y'=4,'c'=2,'x'=4] {'z'}, dimensions={0} | all-to-all | bytes 32768 | tf_op jit(solution)/shard_map/all_to_all | solution.py:310
  226.0 0.6 reduce_sum.34
  (6 shorter events, 0.1 us)
Async XLA Ops:
  40.5 5.8 %copy-start.3 = (f32[3,128]{1,0:T(4,128)S(1)}, f32[3,128]{1,0:T(4,128)}, u32[]{:S(2)}) copy-start(f32[3,128]{1,0:T(4,128)} %param.11) | copy-start | bytes 4612
  40.5 5.9 %copy-start.4 = (f32[3,128]{1,0:T(4,128)S(1)}, f32[3,128]{1,0:T(4,128)}, u32[]{:S(2)}) copy-start(f32[3,128]{1,0:T(4,128)} %param.12) | copy-start | bytes 4612
  40.5 6.6 %copy-start.1 = (bf16[1,128,512]{2,1,0:T(8,128)(2,1)S(1)}, bf16[1,128,512]{2,1,0:T(8,128)(2,1)}, u32[]{:S(2)}) copy-start(bf16[1,128,512]{2,1,0:T(8,128)(2,1)} %param.8) | copy-start | bytes 393220
  40.5 6.8 %copy-start.5 = (s32[128,1]{0,1:T(1,128)S(1)}, s32[128,1]{0,1:T(1,128)}, u32[]{:S(2)}) copy-start(s32[128,1]{0,1:T(1,128)} %param.9) | copy-start | bytes 1540
  40.5 124.4 %all-to-all-start.1 = ((bf16[128,2,5,8,128]{4,3,2,1,0:T(8,128)(2,1)}), bf16[128,2,5,8,128]{4,3,2,1,0:T(8,128)(2,1)S(1)}, u32[]{:S(2)}, u32[]{:S(2)}) async-start(bf16[128,2,5,8,128]{4,3,2,1,0:T(8,128)(2,1)} %gather.1), calls=%async_computation.1 | async-start | bytes 5242880 | tf_op jit(solution)/shard_map/all_to_all | solution.py:291
  48.7 4.1 %copy-start.2 = (f32[3,256]{1,0:T(4,128)S(1)}, f32[3,256]{1,0:T(4,128)}, u32[]{:S(2)}) copy-start(f32[3,256]{1,0:T(4,128)} %param.13) | copy-start | bytes 9220
  164.9 1.2 copy-start
